TPU v7x, 256 devices: a whole 4x4x8 slice. The times are simulated.
256 devices in a mesh: tm: 8 (over z), node: 32 (over x, y, core).
Axes of the slice: x: 4, y: 4, z: 8, core: 2. Of those that a mesh axis runs over, the one named last changes fastest.
Arguments:
- memory: float32 [16384, 256], P('node'), may hold values from -6 to 6
- src_slot: int32 [8, 32, 512], P('tm', 'node'), may hold values from 0 to 4095, as said below
- dst_slot: int32 [8, 32, 512], P('tm', 'node'), may hold values from 0 to 4095, as said below
- event_time: float32 [8, 32, 512], P('tm', 'node'), may hold values from 0 to 200
- touched_rows: int32 [8, 32, 32, 128], P('tm', 'node'), may hold values from 0 to 511, as said below
- time_freq: float32 [128], replicated, may hold values from 0.01 to 1
- msg_weight: bfloat16 [640, 256], replicated, may hold values from -0.25 to 0.25
- msg_bias: float32 [256], replicated, may hold values from -3 to 3
- gate_weight: bfloat16 [256, 512], replicated, may hold values from -0.375 to 0.375
- update_bias: float32 [256], replicated, may hold values from -5 to 1
Outputs:
- period_memory: float32 [8, 16384, 256], P('tm', 'node')
Inputs may be any that keep to these rules, and one draw needn't show every extreme that they name: touched_rows[t, o, b] holds 128 distinct rows among the 512 rows that owner o keeps. `src_slot`: slot s of event block b in period t stands for node (s // 128) * 512 + touched_rows[t, s // 128, b, s % 128]. `dst_slot`: read as src_slot.
All inputs are finite; a program needn't handle non-finite values.
Results may differ from a plain program's by a relative error of at most 0.0019.
Values may be sent and summed in bfloat16 or wider, within the bound.
A program may use at most 64 MiB of HBM per device.

v0:
```python
import jax
import jax.numpy as jnp
from jax import lax
from jax.sharding import PartitionSpec as P


def side_by_side(arrays, axis, split_dim, concat_dim, along):
    ends, at = ([], 0)
    for a in arrays[:-1]:
        at += a.shape[along]
        ends.append(at)
    both = jnp.concatenate(arrays, axis=along)
    return tuple(
        jnp.split(
            lax.all_to_all(both, axis, split_axis=split_dim, concat_axis=concat_dim, tiled=True),
            ends,
            axis=along,
        )
    )


def advance(memory_state, pieces):
    updated = pieces[0] * memory_state + pieces[1]
    return (updated, updated)


def one_hot_rows(indices, width):
    return (indices[:, None] == jnp.arange(width, dtype=jnp.int32)[None, :]).astype(jnp.bfloat16)


def summed_over_rows(hot, values):
    upper = values.astype(jnp.bfloat16)
    lower = (values - upper.astype(jnp.float32)).astype(jnp.bfloat16)
    dims = (((0,), (0,)), ((), ()))
    first = lax.dot_general(hot, upper, dims, preferred_element_type=jnp.float32)
    second = lax.dot_general(hot, lower, dims, preferred_element_type=jnp.float32)
    return first + second


def shards(
    memory,
    src_slot,
    dst_slot,
    event_time,
    touched_rows,
    time_freq,
    msg_weight,
    msg_bias,
    gate_weight,
    update_bias,
):
    row_lists = touched_rows[0, 0]
    blocks, capacity = row_lists.shape
    node_rows, breadth = memory.shape
    slot_total = blocks * capacity
    flat_rows = row_lists.reshape(-1)
    row_hot = one_hot_rows(flat_rows, node_rows)
    picked = jnp.dot(
        row_hot, memory.astype(jnp.bfloat16), preferred_element_type=jnp.float32
    ).astype(jnp.bfloat16)
    fetched = lax.all_to_all(
        picked.reshape(blocks, capacity, breadth), "node", split_axis=0, concat_axis=0, tiled=True
    )
    slot_table = fetched.reshape(slot_total, breadth)
    sources = src_slot[0, 0]
    targets = dst_slot[0, 0]
    all_slots = jnp.concatenate([sources, targets])
    slot_hot = one_hot_rows(all_slots, slot_total)
    both_rows = jnp.dot(slot_hot, slot_table, preferred_element_type=jnp.float32).astype(
        jnp.bfloat16
    )
    events = sources.shape[0]
    from_rows = both_rows[:events]
    to_rows = both_rows[events:]
    encoding = jnp.cos(event_time[0, 0][:, None] * time_freq[None, :]).astype(jnp.bfloat16)
    inputs = jnp.concatenate(
        [
            jnp.concatenate([from_rows, to_rows, encoding], 1),
            jnp.concatenate([to_rows, from_rows, encoding], 1),
        ],
        0,
    )
    messages = jax.nn.relu(
        jnp.dot(inputs, msg_weight, preferred_element_type=jnp.float32) + msg_bias
    )
    totals = summed_over_rows(slot_hot, messages)
    counts = jnp.sum(slot_hot, axis=0, dtype=jnp.float32)
    got_totals, got_counts = (
        lax.all_to_all(
            totals.reshape(blocks, capacity, breadth).astype(jnp.bfloat16),
            "node",
            split_axis=0,
            concat_axis=0,
            tiled=True,
        ).astype(jnp.float32),
        lax.all_to_all(
            counts.reshape(blocks, capacity).astype(jnp.bfloat16),
            "node",
            split_axis=0,
            concat_axis=0,
            tiled=True,
        ).astype(jnp.float32),
    )
    node_totals = summed_over_rows(row_hot, got_totals.reshape(slot_total, breadth))
    node_counts = jnp.dot(
        got_counts.reshape(1, slot_total),
        row_hot.astype(jnp.float32),
        precision=lax.Precision.HIGHEST,
    )[0]
    mean_msg = (node_totals / jnp.maximum(node_counts, 1.0)[:, None]).astype(jnp.bfloat16)
    gate_terms = jnp.dot(mean_msg, gate_weight, preferred_element_type=jnp.float32)
    update = jax.nn.sigmoid(gate_terms[:, :breadth] + update_bias)
    candidate = jnp.tanh(gate_terms[:, breadth:])
    touched = (node_counts > 0.0)[:, None]
    keep_rate = jnp.where(touched, 1.0 - update, 1.0)
    write_term = jnp.where(touched, update * candidate, 0.0)
    tm_count = lax.axis_size("tm")
    row_share = node_rows // tm_count
    keep_parts, write_parts = side_by_side(
        (
            keep_rate.reshape(tm_count, row_share, breadth),
            write_term.reshape(tm_count, row_share, breadth),
        ),
        "tm",
        0,
        0,
        1,
    )
    row_start = lax.axis_index("tm") * row_share
    initial = lax.dynamic_slice_in_dim(memory, row_start, row_share, 0)
    final_state, history = lax.scan(advance, initial, (keep_parts, write_parts))
    returned = lax.all_to_all(history, "tm", split_axis=0, concat_axis=0, tiled=True)
    result = returned.reshape(node_rows, breadth)
    return result[None]


def solution(mesh):
    return jax.shard_map(
        shards,
        mesh=mesh,
        in_specs=(
            P("node", None),
            P("tm", "node", None),
            P("tm", "node", None),
            P("tm", "node", None),
            P("tm", "node", None, None),
            P(),
            P(),
            P(),
            P(),
            P(),
        ),
        out_specs=P("tm", "node", None),
        check_vma=False,
    )
```

profile of v0, /device:TPU:1, one launch (start us, length us, event | category | flops | bytes accessed | tf_op | source)
XLA Modules:
  0.0 165.6 jit_solution(5834958183940461739)
XLA Ops:
  0.0 0.0 copy-start
  0.0 4.2 %fusion.13 = bf16[4096,256]{1,0:T(8,128)(2,1)} fusion(s32[4096]{0:T(1024)} %bitcast.45, f32[512,256]{1,0:T(8,128)} %param.12), kind=kOutput, calls=%fused_computation.18 | convolution fusion | flops 1077018624 | bytes 2637824 | tf_op jit(solution)/shard_map/dot_general | solution.py:58
  4.2 0.0 copy-start.2
  4.2 0.0 copy-start.3
  4.2 0.0 copy-start.1
  4.2 0.0 copy-start.5
  4.2 8.7 %all-to-all-start.1 = ((bf16[32,128,256]{2,1,0:T(8,128)(2,1)}), bf16[32,128,256]{2,1,0:T(8,128)(2,1)S(1)}, u32[]{:S(2)}, u32[]{:S(2)}) async-start(bf16[32,128,256]{2,1,0:T(8,128)(2,1)} %bitcast.35), calls=%async_computation.1 | async-start | bytes 4194304 | tf_op jit(solution)/shard_map/all_to_all | solution.py:61
  12.9 0.0 copy-done.2
  12.9 0.0 copy-done.3
  13.0 3.1 %fusion.4 = bf16[4096]{0:T(1024)(128)(2,1)S(1)} fusion(s32[1024]{0:T(1024)S(1)} %pad_add_fusion), kind=kLoop, calls=%fused_computation.8 | loop fusion | flops 12578816 | bytes 12288 | tf_op jit(solution)/shard_map/reduce_sum | solution.py:87
  16.1 0.6 copy.12
  16.7 0.0 copy-done.1
  16.7 0.0 copy-done.5
  16.7 0.9 cosine_convert_fusion
  17.7 23.6 %all-to-all-done.1 = bf16[32,128,256]{2,1,0:T(8,128)(2,1)S(1)} async-done(((bf16[32,128,256]{2,1,0:T(8,128)(2,1)}), bf16[32,128,256]{2,1,0:T(8,128)(2,1)S(1)}, u32[]{:S(2)}, u32[]{:S(2)}) %all-to-all-start.1) | async-done | bytes 2097184 | tf_op jit(solution)/shard_map/all_to_all | solution.py:61
  41.3 4.5 %all-to-all-start = ((bf16[32,1,128]{2,1,0:T(2,128)(2,1)}), bf16[32,1,128]{2,1,0:T(2,128)(2,1)S(1)}, u32[]{:S(2)}, u32[]{:S(2)}) async-start(bf16[32,1,128]{2,1,0:T(2,128)(2,1)} %copy.12), calls=%async_computation | async-start | bytes 32768 | tf_op jit(solution)/shard_map/all_to_all | solution.py:96
  45.8 0.0 copy-start.7
  45.8 3.9 %fusion.31 = bf16[1024,256]{0,1:T(8,128)(2,1)S(1)} fusion(bf16[4096,256]{1,0:T(8,128)(2,1)S(1)} %bitcast.32, s32[1024]{0:T(1024)S(1)} %pad_add_fusion), kind=kOutput, calls=%fused_computation.38 | convolution fusion | flops 2151940096 | bytes 2625536 | tf_op jit(solution)/shard_map/dot_general | solution.py:69
  49.7 0.0 copy-done
  49.7 0.0 copy-done.7
  49.7 0.6 fusion.19
  50.3 4.7 %fusion = f32[4096,256]{1,0:T(8,128)S(1)} fusion(s32[1024]{0:T(1024)S(1)} %pad_add_fusion, f32[1024,256]{1,0:T(8,128)S(1)} %fusion.19), kind=kOutput, calls=%fused_computation.4 | convolution fusion | flops 2152726528 | bytes 5246976 | tf_op jit(solution)/shard_map/dot_general | solution.py:36
  55.1 6.3 %fusion.14 = bf16[4096,256]{1,0:T(8,128)(2,1)} fusion(f32[4096,256]{1,0:T(8,128)S(1)} %fusion, s32[1024]{0:T(1024)S(1)} %pad_add_fusion, f32[1024,256]{1,0:T(8,128)S(1)} %fusion.19), kind=kOutput, calls=%fused_computation.19 | convolution fusion | flops 2154037248 | bytes 7344128 | tf_op jit(solution)/shard_map/dot_general | solution.py:35
  61.4 0.0 copy-start.6
  61.4 0.0 all-to-all-done
  61.4 7.6 %all-to-all-start.2 = ((bf16[32,128,256]{2,1,0:T(8,128)(2,1)}), bf16[32,128,256]{2,1,0:T(8,128)(2,1)S(1)}, u32[]{:S(2)}, u32[]{:S(2)}) async-start(bf16[32,128,256]{2,1,0:T(8,128)(2,1)} %bitcast.11), calls=%async_computation.2 | async-start | bytes 4194304 | tf_op jit(solution)/shard_map/all_to_all | solution.py:89
  69.0 0.0 copy-done.6
  69.0 1.4 fusion.8
  70.4 26.9 %all-to-all-done.2 = bf16[32,128,256]{2,1,0:T(8,128)(2,1)S(1)} async-done(((bf16[32,128,256]{2,1,0:T(8,128)(2,1)}), bf16[32,128,256]{2,1,0:T(8,128)(2,1)S(1)}, u32[]{:S(2)}, u32[]{:S(2)}) %all-to-all-start.2) | async-done | bytes 2097184 | tf_op jit(solution)/shard_map/all_to_all | solution.py:89
  97.3 3.7 %fusion.6 = f32[512,256]{1,0:T(8,128)} fusion(bf16[4096,256]{1,0:T(8,128)(2,1)S(1)} %bitcast.33, s32[4096]{0:T(1024)S(1)} %bitcast.47), kind=kOutput, calls=%fused_computation.11 | convolution fusion | flops 1075838976 | bytes 2637824 | tf_op jit(solution)/shard_map/dot_general | solution.py:35
  101.1 0.0 copy-start.4
  101.1 4.4 %fusion.35 = f32[512,512]{1,0:T(8,128)S(1)} fusion(bf16[256,512]{1,0:T(8,128)(2,1)} %param.20, f32[512,256]{1,0:T(8,128)} %fusion.6, bf16[4096,256]{1,0:T(8,128)(2,1)S(1)} %bitcast.34, s32[4096]{0:T(1024)S(1)} %bitcast.48, f32[512]{0:T(512)S(1)} %broadcast_maximum_fusion), kind=kOutput, calls=%fused_computation.42 | convolution fusion | flops 1213595648 | bytes 3950592 | tf_op jit(solution)/shard_map/dot_general | solution.py:111
  105.4 0.0 copy-done.4
  105.4 0.2 subtract_select_fusion
  105.7 1.1 pad_maximum_fusion
  106.8 8.2 %all-to-all-start.3 = ((f32[8,128,256]{2,1,0:T(8,128)}), f32[8,128,256]{2,1,0:T(8,128)S(1)}, u32[]{:S(2)}, u32[]{:S(2)}) async-start(f32[8,128,256]{2,1,0:T(8,128)} %pad_maximum_fusion), calls=%async_computation.3 | async-start | bytes 2097152 | tf_op jit(solution)/shard_map/all_to_all | solution.py:15
  115.0 0.8 constant_dynamic-slice_fusion
  115.8 28.3 %all-to-all-done.3 = f32[8,128,256]{2,1,0:T(8,128)S(1)} async-done(((f32[8,128,256]{2,1,0:T(8,128)}), f32[8,128,256]{2,1,0:T(8,128)S(1)}, u32[]{:S(2)}, u32[]{:S(2)}) %all-to-all-start.3) | async-done | bytes 1048608 | tf_op jit(solution)/shard_map/all_to_all | solution.py:15
  144.2 0.1 fusion.48
  144.3 0.3 while.12
  144.6 20.2 %all_to_all.26 = f32[8,64,256]{2,1,0:T(8,128)S(1)} all-to-all(f32[8,64,256]{2,1,0:T(8,128)S(1)} %get-tuple-element.32), channel_id=1, replica_groups=mesh['tm'=8,'node'=32] {'tm'}, dimensions={0} | all-to-all | bytes 1048576 | tf_op jit(solution)/shard_map/all_to_all | solution.py:132
  164.8 0.8 copy.26
  (13 shorter events, 0.2 us)
Async XLA Ops:
  0.0 49.7 %copy-start = (bf16[640,256]{1,0:T(8,128)(2,1)S(1)}, bf16[640,256]{1,0:T(8,128)(2,1)}, u32[]{:S(2)}) copy-start(bf16[640,256]{1,0:T(8,128)(2,1)} %param.18) | copy-start | bytes 983044
  4.2 8.7 %copy-start.2 = (s32[1,1,512]{2,1,0:T(1,128)S(1)}, s32[1,1,512]{2,1,0:T(1,128)}, u32[]{:S(2)}) copy-start(s32[1,1,512]{2,1,0:T(1,128)} %param.14) | copy-start | bytes 6148
  4.2 8.8 %copy-start.3 = (s32[1,1,512]{2,1,0:T(1,128)S(1)}, s32[1,1,512]{2,1,0:T(1,128)}, u32[]{:S(2)}) copy-start(s32[1,1,512]{2,1,0:T(1,128)} %param.13) | copy-start | bytes 6148
  4.2 12.5 %copy-start.1 = (f32[1,1,512]{2,1,0:T(1,128)S(1)}, f32[1,1,512]{2,1,0:T(1,128)}, u32[]{:S(2)}) copy-start(f32[1,1,512]{2,1,0:T(1,128)} %param.15) | copy-start | bytes 6148
  4.2 12.5 %copy-start.5 = (f32[128]{0:T(128)S(1)}, f32[128]{0:T(128)}, u32[]{:S(2)}) copy-start(f32[128]{0:T(128)} %param.17) | copy-start | bytes 1540
  4.2 37.1 %all-to-all-start.1 = ((bf16[32,128,256]{2,1,0:T(8,128)(2,1)}), bf16[32,128,256]{2,1,0:T(8,128)(2,1)S(1)}, u32[]{:S(2)}, u32[]{:S(2)}) async-start(bf16[32,128,256]{2,1,0:T(8,128)(2,1)} %bitcast.35), calls=%async_computation.1 | async-start | bytes 4194304 | tf_op jit(solution)/shard_map/all_to_all | solution.py:61
  41.3 20.1 %all-to-all-start = ((bf16[32,1,128]{2,1,0:T(2,128)(2,1)}), bf16[32,1,128]{2,1,0:T(2,128)(2,1)S(1)}, u32[]{:S(2)}, u32[]{:S(2)}) async-start(bf16[32,1,128]{2,1,0:T(2,128)(2,1)} %copy.12), calls=%async_computation | async-start | bytes 32768 | tf_op jit(solution)/shard_map/all_to_all | solution.py:96
  45.8 4.0 %copy-start.7 = (f32[256]{0:T(256)S(1)}, f32[256]{0:T(256)}, u32[]{:S(2)}) copy-start(f32[256]{0:T(256)} %param.19) | copy-start | bytes 3076
  61.4 7.6 %copy-start.6 = (s32[1,1,32,128]{3,2,1,0:T(8,128)S(1)}, s32[1,1,32,128]{3,2,1,0:T(8,128)}, u32[]{:S(2)}) copy-start(s32[1,1,32,128]{3,2,1,0:T(8,128)} %param.16) | copy-start | bytes 49156
  61.4 36.0 %all-to-all-start.2 = ((bf16[32,128,256]{2,1,0:T(8,128)(2,1)}), bf16[32,128,256]{2,1,0:T(8,128)(2,1)S(1)}, u32[]{:S(2)}, u32[]{:S(2)}) async-start(bf16[32,128,256]{2,1,0:T(8,128)(2,1)} %bitcast.11), calls=%async_computation.2 | async-start | bytes 4194304 | tf_op jit(solution)/shard_map/all_to_all | solution.py:89
  101.1 4.4 %copy-start.4 = (f32[256]{0:T(256)S(1)}, f32[256]{0:T(256)}, u32[]{:S(2)}) copy-start(f32[256]{0:T(256)} %param.21) | copy-start | bytes 3076
  106.8 37.4 %all-to-all-start.3 = ((f32[8,128,256]{2,1,0:T(8,128)}), f32[8,128,256]{2,1,0:T(8,128)S(1)}, u32[]{:S(2)}, u32[]{:S(2)}) async-start(f32[8,128,256]{2,1,0:T(8,128)} %pad_maximum_fusion), calls=%async_computation.3 | async-start | bytes 2097152 | tf_op jit(solution)/shard_map/all_to_all | solution.py:15
where the time goes:
time: 166 us
  waiting for transfers between devices  78.9 us (48%)
  matrix products  29.2 us (18%)
  starting transfers between devices  29 us (17%)
  blocking collectives  20.2 us (12%)
  other arithmetic  5.58 us (3%)
  local copies, waits for them, and re-layouts  2.42 us (1%)
    all_to_all x1, waiting for transfers between devices, side_by_side(): lax.all_to_all(both, axis, split_axis=split_dim, concat_axis=concat_dim,...  28.3 us
    all_to_all x1, waiting for transfers between devices, shards(): lax.all_to_all(totals.reshape(blocks, capacity, breadth).astype(jnp.bfloa...  26.9 us
    all_to_all x1, waiting for transfers between devices, shards(): lax.all_to_all(picked.reshape(blocks, capacity, breadth), 'node', split_a...  23.6 us
    all_to_all x1, blocking collectives, shards(): lax.all_to_all(history, 'tm', split_axis=0, concat_axis=0, tiled=True)  20.2 us
    dot_general x2, matrix products, summed_over_rows(): lax.dot_general(hot, upper, dims, preferred_element_type=jnp.float32)  10 us
    all_to_all x1, starting transfers between devices, shards(): lax.all_to_all(picked.reshape(blocks, capacity, breadth), 'node', split_a...  8.72 us
    all_to_all x1, starting transfers between devices, side_by_side(): lax.all_to_all(both, axis, split_axis=split_dim, concat_axis=concat_dim,...  8.19 us
    all_to_all x1, starting transfers between devices, shards(): lax.all_to_all(totals.reshape(blocks, capacity, breadth).astype(jnp.bfloa...  7.61 us
  transfers between devices with their start and end apart: 4, of which 3 were waited for; matrix products, arithmetic and copies ran while one was open for 14% of the time, Pallas kernels for 0%

commit v1 on v0

v1 whole, which is shorter than its diff:
```python
import functools

import jax
import jax.numpy as jnp
from jax import lax
from jax.experimental import pallas as pl
from jax.experimental.pallas import tpu as pltpu
from jax.sharding import PartitionSpec as P

MESH = pl.DeviceIdType.MESH
F32 = jnp.float32
BF16 = jnp.bfloat16
NT = (((1,), (1,)), ((), ()))
NN = (((1,), (0,)), ((), ()))

PERIODS = 8
OWNERS = 32
ROWS = 512
WIDTH = 256
TERMS = 1024
SHARE = ROWS // PERIODS
BLOCKS = PERIODS * OWNERS
CHUNK = 256


def dot(a, b, dims=NN):
    return lax.dot_general(a, b, dims, preferred_element_type=F32)


def iota(shape, dim):
    return lax.broadcasted_iota(jnp.int32, shape, dim)


def where01(mask):
    return jnp.where(mask, 1.0, 0.0).astype(BF16)


def sorted_terms(slots, times, lists):
    lane = iota((TERMS, 128), 1)
    owner = slots >> 7
    table = jnp.concatenate([(lists - 256).astype(F32), jnp.zeros((128 - OWNERS, 128), F32)], 0)
    per_owner = dot(where01(owner == lane), table.astype(BF16))
    picked = jnp.where((slots & 127) == lane, per_owner, 0.0).astype(BF16)
    ones = jnp.ones((128, 128), BF16)
    row = dot(picked, ones).astype(jnp.int32) + 256
    node = owner * ROWS + row
    bucket = (node >> 6).astype(F32)
    rest = (node & 63).astype(F32)
    eighth = jnp.full((8, 128), 1.0 / 128.0, BF16)
    bucket_row = dot(eighth, bucket.astype(BF16), NT)
    rest_row = dot(eighth, rest.astype(BF16), NT)
    key_col = bucket * TERMS + iota((TERMS, 128), 0).astype(F32)
    key_row = bucket_row * TERMS + iota((8, TERMS), 1).astype(F32)
    below = jnp.zeros((TERMS, 128), F32)
    for q in range(8):
        part = jnp.broadcast_to(key_row[0:1, 128 * q : 128 * (q + 1)], (TERMS, 128))
        below = below + jnp.where(part < key_col, 1.0, 0.0)
    place = dot(below.astype(BF16), ones).astype(jnp.int32)
    half = TERMS // 2
    other_bucket = jnp.concatenate([bucket_row[:, half:], bucket_row[:, :half]], 1)
    other_rest = jnp.concatenate([rest_row[:, half:], rest_row[:, :half]], 1)
    time = jnp.broadcast_to(jnp.concatenate([times, times], 1), (8, TERMS))
    t1 = time.astype(BF16).astype(F32)
    t2 = (time - t1).astype(BF16).astype(F32)
    t3 = time - t1 - t2
    which = iota((8, TERMS), 0)
    meta = jnp.zeros((8, TERMS), F32)
    for k, piece in enumerate((bucket_row, rest_row, other_bucket, other_rest, t1, t2, t3)):
        meta = jnp.where(which == k, piece, meta)
    meta = meta.astype(BF16)
    rows = []
    for q in range(8):
        out = dot(meta, where01(place == lane + 128 * q))
        whole = out.astype(jnp.int32)
        own = whole[0:1] * 64 + whole[1:2]
        other = whole[2:3] * 64 + whole[3:4]
        rows.append(((own << 14) | other, out[4:5] + out[5:6] + out[6:7]))
    return rows


class Gather:
    OPS = 36

    def __init__(self, ref, top, bottom, full, first, base, sems, at):
        self.ref, self.top, self.bottom, self.full = ref, top, bottom, full
        self.first, self.base, self.sems, self.at = first, base, sems, at
        self.started = {}

    def node(self, du, dv, flip=False):
        t, x, y, c = self.at
        dx, dy = (du, dv) if self.first == 0 else (dv, du)
        core = 1 - c if flip else c
        return (lax.rem(x + dx + 4, 4) * 4 + lax.rem(y + dy + 4, 4)) * 2 + core

    def start(self, op, du, dv, part, to):
        piece = self.ref.at[(self.node(du, dv),) + part]
        copy = pltpu.make_async_remote_copy(
            src_ref=piece,
            dst_ref=piece,
            send_sem=self.sems.at[0, self.base + op],
            recv_sem=self.sems.at[1, self.base + op],
            device_id=(self.at[0], to),
            device_id_type=MESH,
        )
        copy.start()
        self.started[op] = copy

    def wait(self, op):
        self.started[op].wait_recv()

    def share(self, k, du, dv):
        self.start(20 + k, du, dv, self.full, self.node(0, 0, True))

    def second(self, i, du):
        self.start(4 + 4 * i, du, 0, self.full, self.node(0, 1))
        self.start(5 + 4 * i, du, 0, self.full, self.node(0, -1))
        self.share(4 * i, du, 0)

    def begin(self):
        self.start(0, 0, 0, self.full, self.node(1, 0))
        self.start(1, 0, 0, self.full, self.node(-1, 0))
        self.second(0, 0)

    def near(self):
        self.wait(0)
        self.start(2, -1, 0, self.top, self.node(1, 0))
        self.second(1, -1)
        self.wait(1)
        self.start(3, 1, 0, self.bottom, self.node(-1, 0))
        self.second(2, 1)

    def far(self):
        self.wait(2)
        self.wait(3)
        self.second(3, 2)

    def column_near(self, i, du):
        self.wait(4 + 4 * i)
        self.start(6 + 4 * i, du, -1, self.top, self.node(0, 1))
        self.share(4 * i + 1, du, -1)
        self.wait(5 + 4 * i)
        self.start(7 + 4 * i, du, 1, self.bottom, self.node(0, -1))
        self.share(4 * i + 2, du, 1)

    def column_far(self, i, du):
        self.wait(6 + 4 * i)
        self.wait(7 + 4 * i)
        self.share(4 * i + 3, du, 2)

    def finish(self):
        for k in range(16):
            self.wait(20 + k)
        for copy in self.started.values():
            copy.wait_send()


def spread_kernel(
    memory, slots, times, lists, table, meta, time, block_lists, sems, list_sems, share_sems
):
    t = lax.axis_index("tm")
    o = lax.axis_index("node")
    x, y, c = o // 8, lax.rem(o // 2, 4), lax.rem(o, 2)
    at = (t, x, y, c)
    barrier = pltpu.get_barrier_semaphore()

    def greet(k, carry):
        pl.semaphore_signal(
            barrier, inc=1, device_id=(t, lax.rem(o + k, OWNERS)), device_id_type=MESH
        )
        return carry

    def greet_periods(k, carry):
        pl.semaphore_signal(
            barrier, inc=1, device_id=(lax.rem(t + k, PERIODS), o), device_id_type=MESH
        )
        return carry

    lax.fori_loop(1, OWNERS, greet, 0)
    lax.fori_loop(1, PERIODS, greet_periods, 0)
    table[pl.ds(o, 1)] = memory[...].astype(BF16)[None]
    block_lists[pl.ds(o, 1)] = lists[pl.ds(o, 1)]
    pl.semaphore_wait(barrier, OWNERS - 1 + PERIODS - 1)

    def list_copy(k):
        to = lax.rem(o + k, OWNERS)
        return pltpu.make_async_remote_copy(
            src_ref=lists.at[to],
            dst_ref=block_lists.at[o],
            send_sem=list_sems.at[0, k],
            recv_sem=list_sems.at[1, k],
            device_id=(t, to),
            device_id_type=MESH,
        )

    def start_list(k, carry):
        list_copy(k).start()
        return carry

    def wait_list(k, carry):
        list_copy(k).wait()
        return carry

    lax.fori_loop(1, OWNERS, start_list, 0)

    def halves(ref, size, step, first, base):
        return Gather(
            ref,
            (pl.ds(step, size // 2),),
            (pl.ds(step + size // 2, size // 2),),
            (pl.ds(step, size),),
            first,
            base,
            sems,
            at,
        )

    n = Gather.OPS
    big = (halves(table, 256, 0, 0, 0), halves(table, 256, 256, 1, n))
    small = (halves(meta, 8, 0, 0, 2 * n), halves(time, 8, 0, 1, 3 * n))
    columns = ((0, 0), (1, -1), (2, 1), (3, 2))
    for g in big:
        g.begin()
    lax.fori_loop(1, OWNERS, wait_list, 0)
    rows = sorted_terms(slots[...], times[...], block_lists[:, 0, :])
    for q, (meta_row, time_row) in enumerate(rows):
        meta[o, t, pl.ds(q, 1), :] = meta_row
        time[o, t, pl.ds(q, 1), :] = time_row
    for g in big:
        g.near()
    sent = []
    for k in range(1, PERIODS):
        for j, ref in enumerate((meta, time)):
            copy = pltpu.make_async_remote_copy(
                src_ref=ref.at[o, t],
                dst_ref=ref.at[o, t],
                send_sem=share_sems.at[0, j, k],
                recv_sem=share_sems.at[1, j, k],
                device_id=(lax.rem(t + k, PERIODS), o),
                device_id_type=MESH,
            )
            copy.start()
            sent.append(copy)
    for g in big:
        g.far()
    for g in big:
        g.column_near(*columns[0])
    for copy in sent:
        copy.wait()
    for g in small:
        g.begin()
    for col in columns[1:3]:
        for g in big:
            g.column_near(*col)
    for g in small:
        g.near()
    for g in big:
        g.column_near(*columns[3])
    for g in small:
        g.far()
    for col in columns[:3]:
        for g in big:
            g.column_far(*col)
        for g in small:
            g.column_near(*col)
    for g in big:
        g.column_far(*columns[3])
    for g in small:
        g.column_near(*columns[3])
    for col in columns:
        for g in small:
            g.column_far(*col)
    for g in big + small:
        g.finish()


def spread(memory, slots, times, lists):
    return pl.pallas_call(
        spread_kernel,
        out_shape=(
            jax.ShapeDtypeStruct((OWNERS, ROWS, WIDTH), BF16),
            jax.ShapeDtypeStruct((OWNERS, PERIODS, 8, 128), jnp.int32),
            jax.ShapeDtypeStruct((OWNERS, PERIODS, 8, 128), F32),
        ),
        in_specs=[pl.BlockSpec(memory_space=pltpu.VMEM)] * 4,
        out_specs=[pl.BlockSpec(memory_space=pltpu.VMEM)] * 3,
        scratch_shapes=[
            pltpu.VMEM((OWNERS, 1, 128), jnp.int32),
            pltpu.SemaphoreType.DMA((2, 4 * Gather.OPS)),
            pltpu.SemaphoreType.DMA((2, OWNERS)),
            pltpu.SemaphoreType.DMA((2, 2, PERIODS)),
        ],
        compiler_params=pltpu.CompilerParams(
            collective_id=0, has_side_effects=True, vmem_limit_bytes=40 * 2**20
        ),
        name="spread",
    )(memory, slots, times, lists)


def message_kernel(
    table, meta, time, freq, weight, bias, totals, counts,
    wide, window, window_time, pieces, rows_v, rows_s, index_v, index_s, gathered, sem,
):
    bucket = lax.axis_index("node") * PERIODS + lax.axis_index("tm")

    def widen(i, carry):
        at = pl.multiple_of(i * 256, 256)
        wide[pl.ds(at, 256), :] = table[pl.ds(at, 256), :].astype(F32)
        return carry

    lax.fori_loop(0, OWNERS * ROWS // 256, widen, 0)
    totals[...] = jnp.zeros_like(totals)
    counts[...] = jnp.zeros_like(counts)
    start_parts, end_parts = [], []
    for i in range(8):
        own = meta[pl.ds(32 * i, 32)] >> 20
        start_parts.append(jnp.sum(jnp.where(own < bucket, 1.0, 0.0), axis=1))
        end_parts.append(jnp.sum(jnp.where(own <= bucket, 1.0, 0.0), axis=1))
    ones_row = jnp.ones((8, 128), BF16)
    start = dot(ones_row, jnp.concatenate(start_parts, 0).astype(BF16), NT)
    end = dot(ones_row, jnp.concatenate(end_parts, 0).astype(BF16), NT)
    upper = where01(iota((BLOCKS, BLOCKS), 0) < iota((BLOCKS, BLOCKS), 1))
    own_rows = wide[pl.ds(pl.multiple_of(bucket * SHARE, SHARE), SHARE), :].astype(BF16)
    own_rows = jnp.concatenate([own_rows, jnp.zeros((128 - SHARE, WIDTH), BF16)], 0)
    ones_wide = jnp.ones((8, BLOCKS), BF16)
    ones_col = jnp.ones((BLOCKS, 128), BF16)
    freqs = jnp.broadcast_to(freq[...], (CHUNK, 128))
    biases = jnp.broadcast_to(bias[...], (CHUNK, WIDTH))
    longest = jnp.max(end - start)

    def one_round(r, carry):
        begin = start + (r * 128).astype(F32)
        size = jnp.clip(end - begin, 0.0, 128.0)
        before = dot(size.astype(BF16), upper)
        which = iota((8, BLOCKS), 0)
        begin_i = begin.astype(jnp.int32)
        rows_v[...] = jnp.where(which == 0, begin_i, (before + size).astype(jnp.int32))
        copy = pltpu.make_async_copy(rows_v, rows_s, sem)
        copy.start()
        copy.wait()
        total = rows_s[1, BLOCKS - 1]

        def fetch(i, carry):
            for u in range(8):
                b = i * 8 + u
                at = rows_s[0, b] >> 7
                a0 = jnp.minimum(at, 7)
                a1 = jnp.minimum(at + 1, 7)
                window[b, 0] = meta[b, a0]
                window[b, 1] = meta[b, a1]
                window_time[b, 0] = time[b, a0]
                window_time[b, 1] = time[b, a1]
            return carry

        lax.fori_loop(0, BLOCKS // 8, fetch, 0)
        for j in range(2):
            m = window[:, j, :]
            w = window_time[:, j, :]
            period = iota((BLOCKS, 128), 0) & 7
            seg = period * SHARE + ((m >> 14) & 63) - 256
            t1 = w.astype(BF16).astype(F32)
            t2 = (w - t1).astype(BF16).astype(F32)
            t3 = w - t1 - t2
            for k, piece in enumerate(
                (seg.astype(F32), ((m >> 6) & 255).astype(F32), (m & 63).astype(F32), t1, t2, t3)
            ):
                pieces[:, 256 * k + 128 * j : 256 * k + 128 * (j + 1)] = piece.astype(BF16)
        offset = (begin_i & 127).astype(F32) - before

        def one_chunk(ch, carry):
            p = (ch * CHUNK).astype(F32) + iota((CHUNK, BLOCKS), 0).astype(F32)
            low = jnp.broadcast_to(before[0:1], (CHUNK, BLOCKS))
            high = low + jnp.broadcast_to(size[0:1], (CHUNK, BLOCKS))
            hit = (low <= p) & (p < high)
            shift = jnp.sum(
                jnp.where(hit, jnp.broadcast_to(offset[0:1], (CHUNK, BLOCKS)), 0.0),
                axis=1,
                keepdims=True,
            )
            found = dot(where01(hit), pieces[...])
            here = (p + shift) == iota((CHUNK, BLOCKS), 1).astype(F32)
            chosen = [
                jnp.where(here, found[:, 256 * k : 256 * (k + 1)], 0.0).astype(BF16)
                for k in range(6)
            ]
            other = dot(ones_wide, chosen[1], NT) * 64.0 + dot(ones_wide, chosen[2], NT)
            index_v[...] = other.astype(jnp.int32)
            copy = pltpu.make_async_copy(index_v, index_s, sem)
            copy.start()
            seg_row = dot(ones_wide, chosen[0], NT) + 256.0
            lane_p = (ch * CHUNK + iota((8, CHUNK), 1)).astype(F32)
            seg_row = jnp.where(lane_p < total.astype(F32), seg_row, -1.0)
            seg_col = dot(chosen[0], ones_col).astype(jnp.int32) + 256
            own_hot = where01((seg_col & 63) == iota((CHUNK, 128), 1))
            own = dot(own_hot, own_rows).astype(BF16)
            moment = dot(chosen[3], ones_col) + dot(chosen[4], ones_col) + dot(chosen[5], ones_col)
            encoding = jnp.cos(moment * freqs).astype(BF16)
            part = dot(own, weight[pl.ds(0, WIDTH), :]) + dot(
                encoding, weight[pl.ds(2 * WIDTH, 128), :]
            )
            seg_hot = where01(
                iota((ROWS, CHUNK), 0).astype(F32) == jnp.broadcast_to(seg_row[0:1], (ROWS, CHUNK))
            )
            copy.wait()

            def pick(i, carry):
                for u in range(8):
                    q = i * 8 + u
                    gathered[pl.ds(q, 1), :] = wide[pl.ds(index_s[0, q], 1), :]
                return carry

            lax.fori_loop(0, CHUNK // 8, pick, 0)
            part = part + dot(gathered[...].astype(BF16), weight[pl.ds(WIDTH, WIDTH), :])
            message = jnp.maximum(part + biases, 0.0)
            upper_part = message.astype(BF16)
            lower_part = (message - upper_part.astype(F32)).astype(BF16)
            totals[...] += dot(seg_hot, upper_part) + dot(seg_hot, lower_part)
            counts[...] += dot(seg_hot, ones_col)
            return carry

        lax.fori_loop(0, (total + CHUNK - 1) // CHUNK, one_chunk, 0)
        return carry

    rounds = (longest.astype(jnp.int32) + 127) // 128
    lax.fori_loop(0, rounds, one_round, 0)


def messages(table, meta, time, freq, weight, bias):
    return pl.pallas_call(
        message_kernel,
        out_shape=(
            jax.ShapeDtypeStruct((ROWS, WIDTH), F32),
            jax.ShapeDtypeStruct((ROWS, 128), F32),
        ),
        in_specs=[pl.BlockSpec(memory_space=pltpu.VMEM)] * 6,
        out_specs=[pl.BlockSpec(memory_space=pltpu.VMEM)] * 2,
        scratch_shapes=[
            pltpu.VMEM((OWNERS * ROWS, WIDTH), F32),
            pltpu.VMEM((BLOCKS, 2, 128), jnp.int32),
            pltpu.VMEM((BLOCKS, 2, 128), F32),
            pltpu.VMEM((BLOCKS, 6 * 256), BF16),
            pltpu.VMEM((8, BLOCKS), jnp.int32),
            pltpu.SMEM((8, BLOCKS), jnp.int32),
            pltpu.VMEM((8, CHUNK), jnp.int32),
            pltpu.SMEM((8, CHUNK), jnp.int32),
            pltpu.VMEM((CHUNK, WIDTH), F32),
            pltpu.SemaphoreType.DMA,
        ],
        compiler_params=pltpu.CompilerParams(vmem_limit_bytes=44 * 2**20),
        name="messages",
    )(table, meta, time, freq, weight, bias)


def update_kernel(memory, totals, counts, weight, bias, result, history, arrived, sems):
    t = lax.axis_index("tm")
    o = lax.axis_index("node")
    barrier = pltpu.get_barrier_semaphore()
    for k in range(1, PERIODS):
        pl.semaphore_signal(
            barrier, inc=1, device_id=(lax.rem(t + k, PERIODS), o), device_id_type=MESH
        )
    count = counts[...]
    count = jnp.concatenate([count, count], 1)
    mean = (totals[...] / jnp.maximum(count, 1.0)).astype(BF16)
    gates = dot(mean, weight[...])
    rate = jax.nn.sigmoid(gates[:, :WIDTH] + bias[...])
    candidate = jnp.tanh(gates[:, WIDTH:])
    touched = count > 0.0
    keep = jnp.where(touched, 1.0 - rate, 1.0)
    write = jnp.where(touched, rate * candidate, 0.0)
    mine = pl.ds(pl.multiple_of(t * SHARE, SHARE), SHARE)
    state = memory[mine, :]
    for k in range(PERIODS):
        rows = slice(k * SHARE, (k + 1) * SHARE)
        state = keep[rows] * state + write[rows]
        history[k] = state.astype(BF16)

        @pl.when(t == k)
        def _():
            result[mine, :] = state

    pl.semaphore_wait(barrier, PERIODS - 1)
    copies = []
    for k in range(1, PERIODS):
        to = lax.rem(t + k, PERIODS)
        copy = pltpu.make_async_remote_copy(
            src_ref=history.at[to],
            dst_ref=arrived.at[t],
            send_sem=sems.at[0, k],
            recv_sem=sems.at[1, k],
            device_id=(to, o),
            device_id_type=MESH,
        )
        copy.start()
        copies.append(copy)
    for k in (1, 7, 2, 6, 3, 5, 4):
        copies[k - 1].wait_recv()
        source = lax.rem(t + PERIODS - k, PERIODS)
        result[pl.ds(pl.multiple_of(source * SHARE, SHARE), SHARE), :] = arrived[source].astype(F32)
    for copy in copies:
        copy.wait_send()


def update(memory, totals, counts, weight, bias):
    return pl.pallas_call(
        update_kernel,
        out_shape=jax.ShapeDtypeStruct((ROWS, WIDTH), F32),
        in_specs=[pl.BlockSpec(memory_space=pltpu.VMEM)] * 5,
        out_specs=pl.BlockSpec(memory_space=pltpu.VMEM),
        scratch_shapes=[
            pltpu.VMEM((PERIODS, SHARE, WIDTH), BF16),
            pltpu.VMEM((PERIODS, SHARE, WIDTH), BF16),
            pltpu.SemaphoreType.DMA((2, PERIODS)),
        ],
        compiler_params=pltpu.CompilerParams(collective_id=1, has_side_effects=True),
        name="update",
    )(memory, totals, counts, weight, bias)


def shards(
    memory,
    src_slot,
    dst_slot,
    event_time,
    touched_rows,
    time_freq,
    msg_weight,
    msg_bias,
    gate_weight,
    update_bias,
):
    slots = jnp.concatenate([src_slot[0, 0], dst_slot[0, 0]])
    slots = jnp.broadcast_to(slots[:, None], (TERMS, 128))
    table, meta, time = spread(
        memory, slots, event_time[0], touched_rows.reshape(OWNERS, 1, 128)
    )
    totals, counts = messages(
        table.reshape(OWNERS * ROWS, WIDTH),
        meta.reshape(BLOCKS, 8, 128),
        time.reshape(BLOCKS, 8, 128),
        time_freq[None],
        msg_weight,
        msg_bias[None],
    )
    return update(memory, totals, counts, gate_weight, update_bias[None])[None]


def solution(mesh):
    return jax.shard_map(
        shards,
        mesh=mesh,
        in_specs=(
            P("node", None),
            P("tm", "node", None),
            P("tm", "node", None),
            P("tm", "node", None),
            P("tm", "node", None, None),
            P(),
            P(),
            P(),
            P(),
            P(),
        ),
        out_specs=P("tm", "node", None),
        check_vma=False,
    )
```

time: 166 us -> 101 us (0.61)
  the two profiles are of different devices: /device:TPU:1 before, /device:TPU:4 now
where the time goes in v1:
time: 101 us; the launch traced here: 99.7 us
  Pallas kernels  87.4 us (87%)
  local copies, waits for them, and re-layouts  11.5 us (11%)
    pallas_call x1, Pallas kernels, spread(): pl.pallas_call(spread_kernel, out_shape=(jax.ShapeDtypeStruct((OWNERS, RO...  48.2 us
    pallas_call x1, Pallas kernels, messages(): pl.pallas_call(message_kernel, out_shape=(jax.ShapeDtypeStruct((ROWS, WID...  25.4 us
    pallas_call x1, Pallas kernels, update(): pl.pallas_call(update_kernel, out_shape=jax.ShapeDtypeStruct((ROWS, WIDTH...  13.7 us
    unnamed x19, local copies, waits for them, and re-layouts  11.3 us

profile of v1, /device:TPU:4, one launch (start us, length us, event | category | flops | bytes accessed | tf_op | source)
XLA Modules:
  0.0 99.7 jit_solution(13060856056347976320)
XLA Ops:
  0.0 0.7 pad_add_fusion
  0.7 0.2 broadcast_in_dim.18.slots
  0.9 0.0 copy-start.1
  0.9 1.0 %copy-done.1 = f32[512,256]{1,0:T(8,128)S(1)} copy-done((f32[512,256]{1,0:T(8,128)S(1)}, f32[512,256]{1,0:T(8,128)}, u32[]{:S(2)}) %copy-start.1) | copy-done | bytes 524312
  2.0 0.0 copy-start.5
  2.0 0.7 copy-done.5
  2.7 0.0 copy-start.6
  2.7 0.7 copy-done.6
  3.4 48.2 %spread.1 = (bf16[32,512,256]{2,1,0:T(8,128)(2,1)S(1)}, s32[32,8,8,128]{3,2,1,0:T(8,128)S(1)}, f32[32,8,8,128]{3,2,1,0:T(8,128)S(1)}) custom-call(f32[512,256]{1,0:T(8,128)S(1)} %copy-done.1, s32[1024,128]{1,0:T(8,128)S(1)} %broadcast_in_dim.18.slots, f32[1,512]{1,0:T(1,128)S(1)} %bitcast.15, s32[32,1,128]{2,1,0:T(1,128)S(1)} %bitcast.14), custom_call_target="tpu_custom_call" | custom-call | tf_op jit(solution)/shard_map/spread/pallas_call | solution.py:277
  51.6 0.0 copy-start
  51.6 3.2 %copy-done = bf16[32,512,256]{2,1,0:T(8,128)(2,1)} copy-done((bf16[32,512,256]{2,1,0:T(8,128)(2,1)}, bf16[32,512,256]{2,1,0:T(8,128)(2,1)S(1)}, u32[]{:S(2)}) %copy-start) | copy-done | bytes 8388632
  54.8 0.0 copy-start.3
  54.8 1.0 copy-done.3
  55.8 0.0 copy-start.7
  55.8 0.7 copy-done.7
  56.5 0.0 copy-start.8
  56.5 0.7 copy-done.8
  57.1 25.4 %messages.1 = (f32[512,256]{1,0:T(8,128)S(1)}, f32[512,128]{1,0:T(8,128)S(1)}) custom-call(bf16[16384,256]{1,0:T(8,128)(2,1)} %bitcast.11, s32[256,8,128]{2,1,0:T(8,128)S(1)} %bitcast.12, f32[256,8,128]{2,1,0:T(8,128)S(1)} %bitcast.13, f32[1,128]{1,0:T(1,128)S(1)} %bitcast.17, bf16[640,256]{1,0:T(8,128)(2,1)S(1)} %copy-done.3, f32[1,256]{1,0:T(1,128)S(1)} %bitcast.16), custom_call_target="tpu_custom_call" | custom-call | tf_op jit(solution)/shard_map/messages/pallas_call | solution.py:428
  82.6 0.0 copy-start.2
  82.6 0.8 copy-done.2
  83.4 0.0 copy-start.4
  83.4 0.7 copy-done.4
  84.0 13.7 %update.1 = f32[512,256]{1,0:T(8,128)} custom-call(f32[512,256]{1,0:T(8,128)} %memory.3, f32[512,256]{1,0:T(8,128)} %copy-done.2, f32[512,128]{1,0:T(8,128)} %copy-done.4, bf16[256,512]{1,0:T(8,128)(2,1)} %weight.3, f32[1,256]{1,0:T(1,128)} %bitcast.21), custom_call_target="tpu_custom_call" | custom-call | tf_op jit(solution)/shard_map/update/pallas_call | solution.py:504
  97.8 1.9 %copy.12 = f32[1,512,256]{2,1,0:T(8,128)} copy(f32[1,512,256]{2,1,0:T(8,128)} %bitcast.18) | data formatting | bytes 1048576
Async XLA Ops:
  0.9 1.0 %copy-start.1 = (f32[512,256]{1,0:T(8,128)S(1)}, f32[512,256]{1,0:T(8,128)}, u32[]{:S(2)}) copy-start(f32[512,256]{1,0:T(8,128)} %memory.3) | copy-start | bytes 1572868
  2.0 0.7 copy-start.5
  2.7 0.7 copy-start.6
  51.6 3.2 %copy-start = (bf16[32,512,256]{2,1,0:T(8,128)(2,1)}, bf16[32,512,256]{2,1,0:T(8,128)(2,1)S(1)}, u32[]{:S(2)}) copy-start(bf16[32,512,256]{2,1,0:T(8,128)(2,1)S(1)} %get-tuple-element.10) | copy-start | bytes 25165828
  54.8 1.0 copy-start.3
  55.8 0.7 copy-start.7
  56.5 0.7 copy-start.8
  82.6 0.8 copy-start.2
  83.4 0.7 copy-start.4

commit v2 on v1

v2 whole, which is shorter than its diff:
```python
import math

import jax
import jax.numpy as jnp
from jax import lax
from jax.experimental import pallas as pl
from jax.experimental.pallas import tpu as pltpu
from jax.sharding import PartitionSpec as P

MESH = pl.DeviceIdType.MESH
F32 = jnp.float32
BF16 = jnp.bfloat16
NT = (((1,), (1,)), ((), ()))
NN = (((1,), (0,)), ((), ()))

PERIODS = 8
OWNERS = 32
ROWS = 512
WIDTH = 256
TERMS = 1024
SHARE = ROWS // PERIODS
BLOCKS = PERIODS * OWNERS
CHUNK = 512
GROUP = 4
UNROLL = 32


def dot(a, b, dims=NN):
    return lax.dot_general(a, b, dims, preferred_element_type=F32)


def iota(shape, dim):
    return lax.broadcasted_iota(jnp.int32, shape, dim)


def where01(mask):
    return jnp.where(mask, 1.0, 0.0).astype(BF16)


def cosine(angle):
    turns = jnp.floor(angle * (0.5 / math.pi) + 0.5)
    rest = angle - turns * 6.28125
    rest = rest - turns * (2.0 * math.pi - 6.28125)
    square = rest * rest
    value = jnp.full_like(angle, 1.0 / math.factorial(16))
    for k in range(7, -1, -1):
        value = value * square + (-1.0) ** k / math.factorial(2 * k)
    return value


def sorted_terms(sources, targets, times, lists):
    lane = iota((TERMS, 128), 1)
    ones = jnp.ones((128, 128), BF16)
    square = iota((128, 128), 0) == iota((128, 128), 1)
    owners, places = [], []
    for slots in (sources, targets):
        for q in range(4):
            row = jnp.broadcast_to(slots[:, 128 * q : 128 * (q + 1)], (128, 128))
            owners.append(dot(jnp.where(square, row >> 7, 0).astype(F32).astype(BF16), ones))
            places.append(dot(jnp.where(square, row & 127, 0).astype(F32).astype(BF16), ones))
    owner = jnp.concatenate(owners, 0).astype(jnp.int32)
    slot = jnp.concatenate(places, 0).astype(jnp.int32)
    table = jnp.concatenate([(lists - 256).astype(F32), jnp.zeros((128 - OWNERS, 128), F32)], 0)
    per_owner = dot(where01(owner == lane), table.astype(BF16))
    picked = jnp.where(slot == lane, per_owner, 0.0).astype(BF16)
    row = dot(picked, ones).astype(jnp.int32) + 256
    node = owner * ROWS + row
    bucket = (node >> 6).astype(F32)
    rest = (node & 63).astype(F32)
    eighth = jnp.full((8, 128), 1.0 / 128.0, BF16)
    bucket_row = dot(eighth, bucket.astype(BF16), NT)
    rest_row = dot(eighth, rest.astype(BF16), NT)
    key_col = bucket * TERMS + iota((TERMS, 128), 0).astype(F32)
    key_row = bucket_row * TERMS + iota((8, TERMS), 1).astype(F32)
    below = jnp.zeros((TERMS, 128), F32)
    for q in range(8):
        part = jnp.broadcast_to(key_row[0:1, 128 * q : 128 * (q + 1)], (TERMS, 128))
        below = below + jnp.where(part < key_col, 1.0, 0.0)
    place = dot(below.astype(BF16), ones).astype(jnp.int32)
    half = TERMS // 2
    other_bucket = jnp.concatenate([bucket_row[:, half:], bucket_row[:, :half]], 1)
    other_rest = jnp.concatenate([rest_row[:, half:], rest_row[:, :half]], 1)
    time = jnp.broadcast_to(jnp.concatenate([times, times], 1), (8, TERMS))
    t1 = time.astype(BF16).astype(F32)
    t2 = (time - t1).astype(BF16).astype(F32)
    t3 = time - t1 - t2
    which = iota((8, TERMS), 0)
    meta = jnp.zeros((8, TERMS), F32)
    for k, piece in enumerate((bucket_row, rest_row, other_bucket, other_rest, t1, t2, t3)):
        meta = jnp.where(which == k, piece, meta)
    meta = meta.astype(BF16)
    rows = []
    for q in range(8):
        out = dot(meta, where01(place == lane + 128 * q))
        whole = out.astype(jnp.int32)
        own = whole[0:1] * 64 + whole[1:2]
        other = whole[2:3] * 64 + whole[3:4]
        rows.append(((own << 14) | other, out[4:5] + out[5:6] + out[6:7]))
    return rows


class Gather:
    OPS = 36
    COLUMNS = ((0, 0), (1, -1), (2, 1), (3, 2))
    PLACES = (0, -1, 1, 2)

    def __init__(self, ref, start, size, first, base, sems, at, landed=None):
        self.ref = ref
        self.full = (pl.ds(start, size),)
        self.top = (pl.ds(start, size // 2),)
        self.bottom = (pl.ds(start + size // 2, size // 2),)
        self.first, self.base, self.sems, self.at = first, base, sems, at
        self.landed = landed
        self.started = {}

    def node(self, du, dv, flip=False):
        t, x, y, c = self.at
        dx, dy = (du, dv) if self.first == 0 else (dv, du)
        core = 1 - c if flip else c
        return (lax.rem(x + dx + 4, 4) * 4 + lax.rem(y + dy + 4, 4)) * 2 + core

    def land(self, du, dv, flip=False):
        if self.landed is not None:
            self.landed(self.node(du, dv, flip), self.full)

    def start(self, op, du, dv, part, to):
        piece = self.ref.at[(self.node(du, dv),) + part]
        copy = pltpu.make_async_remote_copy(
            src_ref=piece,
            dst_ref=piece,
            send_sem=self.sems.at[0, self.base + op],
            recv_sem=self.sems.at[1, self.base + op],
            device_id=(self.at[0], to),
            device_id_type=MESH,
        )
        copy.start()
        self.started[op] = copy

    def wait(self, op):
        self.started[op].wait_recv()

    def share(self, k, du, dv):
        self.start(20 + k, du, dv, self.full, self.node(0, 0, True))

    def second(self, i, du):
        self.start(4 + 4 * i, du, 0, self.full, self.node(0, 1))
        self.start(5 + 4 * i, du, 0, self.full, self.node(0, -1))
        self.share(4 * i, du, 0)

    def begin(self):
        self.start(0, 0, 0, self.full, self.node(1, 0))
        self.start(1, 0, 0, self.full, self.node(-1, 0))

    def own_second(self):
        self.second(0, 0)

    def near(self):
        self.wait(0)
        self.start(2, -1, 0, self.top, self.node(1, 0))
        self.second(1, -1)
        self.wait(1)
        self.start(3, 1, 0, self.bottom, self.node(-1, 0))
        self.second(2, 1)
        self.land(-1, 0)
        self.land(1, 0)

    def far(self):
        self.wait(2)
        self.wait(3)
        self.second(3, 2)
        self.land(2, 0)

    def column_near(self, i):
        du = self.PLACES[i]
        self.wait(4 + 4 * i)
        self.start(6 + 4 * i, du, -1, self.top, self.node(0, 1))
        self.share(4 * i + 1, du, -1)
        self.wait(5 + 4 * i)
        self.start(7 + 4 * i, du, 1, self.bottom, self.node(0, -1))
        self.share(4 * i + 2, du, 1)
        self.land(du, -1)
        self.land(du, 1)

    def column_far(self, i):
        du = self.PLACES[i]
        self.wait(6 + 4 * i)
        self.wait(7 + 4 * i)
        self.share(4 * i + 3, du, 2)
        self.land(du, 2)

    def shared(self, *ks):
        for k in ks:
            self.wait(20 + k)
            self.land(self.PLACES[k // 4], self.PLACES[k % 4], True)

    def finish(self):
        for copy in self.started.values():
            copy.wait_send()


def spread_kernel(
    memory_h, source_h, target_h, moment_h, lists_h, wide, meta, time,
    memory, source, target, moment, lists, table, block_lists, load_sems, sems, list_sems, share_sems,
):
    t = lax.axis_index("tm")
    o = lax.axis_index("node")
    x, y, c = o // 8, lax.rem(o // 2, 4), lax.rem(o, 2)
    at = (t, x, y, c)
    loads = [
        pltpu.make_async_copy(src, dst, load_sems.at[i])
        for i, (src, dst) in enumerate(
            (
                (memory_h, memory),
                (lists_h, lists),
                (source_h, source),
                (target_h, target),
                (moment_h, moment),
            )
        )
    ]
    for load in loads:
        load.start()
    barrier = pltpu.get_barrier_semaphore()

    def greet(k, carry):
        pl.semaphore_signal(
            barrier, inc=1, device_id=(t, lax.rem(o + k, OWNERS)), device_id_type=MESH
        )
        return carry

    def greet_periods(k, carry):
        pl.semaphore_signal(
            barrier, inc=1, device_id=(lax.rem(t + k, PERIODS), o), device_id_type=MESH
        )
        return carry

    lax.fori_loop(1, OWNERS, greet, 0)
    lax.fori_loop(1, PERIODS, greet_periods, 0)
    for load in loads:
        load.wait()
    table[pl.ds(o, 1)] = memory[...].astype(BF16)[None]
    block_lists[pl.ds(o, 1)] = lists[pl.ds(o, 1)]

    def widen(node, part):
        rows = part[0]
        wide[pl.ds(pl.multiple_of(node * ROWS + rows.start, 64), rows.size), :] = table[
            node, rows, :
        ].astype(F32)

    pl.semaphore_wait(barrier, OWNERS - 1 + PERIODS - 1)

    def list_copy(k):
        to = lax.rem(o + k, OWNERS)
        return pltpu.make_async_remote_copy(
            src_ref=lists.at[to],
            dst_ref=block_lists.at[o],
            send_sem=list_sems.at[0, k],
            recv_sem=list_sems.at[1, k],
            device_id=(t, to),
            device_id_type=MESH,
        )

    def wait_list(k, carry):
        list_copy(k).wait()
        return carry

    for k in FAR_FIRST:
        for core in range(2):
            if k + core:
                list_copy(2 * k + core).start()
    n = Gather.OPS
    big = (
        Gather(table, 0, 256, 0, 0, sems, at, widen),
        Gather(table, 256, 256, 1, n, sems, at, widen),
    )
    chip = o // 2
    pair = (meta, time)

    def list_send(j, piece, to, op):
        copy = pltpu.make_async_remote_copy(
            src_ref=piece,
            dst_ref=piece,
            send_sem=share_sems.at[0, j, op],
            recv_sem=share_sems.at[1, j, op],
            device_id=to,
            device_id_type=MESH,
        )
        copy.start()
        sent[j, op] = copy

    sent = {}

    def plane_send():
        for k in FAR_FIRST[:-1]:
            to = lax.rem(chip + k, 16) * 2 + c
            for j in range(2):
                list_send(j, pair[j].at[c, t, chip], (t, to), k)

    def plane_take():
        for k in range(1, 16):
            for j in range(2):
                sent[j, k].wait_recv()

    def period(step):
        return lax.rem(t + step + PERIODS, PERIODS)

    def ring_start(step):
        whole = step < 3
        for j in range(2):
            if step:
                sent[j, 16 + 2 * (step - 1)].wait_recv()
            up = pair[j].at[c, period(-step)]
            list_send(j, up if whole else up.at[pl.ds(0, 8)], (period(1), o), 16 + 2 * step)
            if step:
                sent[j, 17 + 2 * (step - 1)].wait_recv()
            down = pair[j].at[c, period(step)]
            list_send(j, down if whole else down.at[pl.ds(8, 8)], (period(-1), o), 17 + 2 * step)

    def ring_end():
        for j in range(2):
            sent[j, 22].wait_recv()
            sent[j, 23].wait_recv()

    def partner_send(*steps):
        for step in steps:
            for j in range(2):
                list_send(j, pair[j].at[c, period(step)], (t, o + 1 - 2 * c), 24 + step % 8)

    def partner_take():
        for step in range(8):
            for j in range(2):
                sent[j, 24 + step].wait_recv()

    def own_rows():
        for start in (0, 256):
            widen(o, (pl.ds(start, 256),))

    def sort():
        lax.fori_loop(1, OWNERS, wait_list, 0)
        rows = sorted_terms(source[...], target[...], moment[...], block_lists[:, 0, :])
        for q, (meta_row, time_row) in enumerate(rows):
            meta[c, t, chip, pl.ds(q, 1), :] = meta_row
            time[c, t, chip, pl.ds(q, 1), :] = time_row

    def both(group, step, *numbers):
        for g in group:
            getattr(g, step)(*numbers)

    def run(order):
        for word in order:
            if word == "own":
                own_rows()
            elif word == "sort":
                sort()
            elif word == "plane":
                plane_send()
            elif word == "taken":
                plane_take()
            elif word == "end":
                ring_end()
            elif word == "partner":
                partner_take()
            elif word[0] == "R":
                ring_start(int(word[1]))
            elif word[0] == "P":
                partner_send(*(int(k) for k in word[1:].split(",")))
            else:
                numbers = [int(k) for k in word[2:].split(",") if k]
                step = STEPS[word[1]]
                if step == "shared" or not numbers:
                    both(big, step, *numbers)
                else:
                    for k in numbers:
                        both(big, step, k)

    run(ORDER)
    for g in big:
        g.finish()
    for copy in sent.values():
        copy.wait_send()


FAR_FIRST = (10, 6, 9, 11, 14, 2, 5, 7, 8, 13, 15, 1, 3, 4, 12, 0)
STEPS = {
    "b": "begin",
    "s": "own_second",
    "n": "near",
    "f": "far",
    "c": "column_near",
    "d": "column_far",
    "h": "shared",
}
ORDER = (
    "Mb", "Ms", "own", "sort", "plane", "Mn", "taken", "R0", "P0", "Mf", "Mc0", "R1",
    "P1,-1", "Mc1", "Mh0,4,8", "R2", "P2,-2", "Mc2", "Mh1,2,12", "R3", "P3,-3", "Mc3",
    "Md0", "Mh5,6", "Md1", "Mh9,10", "end", "P4", "Md2", "Mh13,14", "Md3", "Mh3,7,11,15",
    "partner",
)

VMEM = pl.BlockSpec(memory_space=pltpu.VMEM)
HBM = pl.BlockSpec(memory_space=pltpu.HBM)


def in_hbm(*arrays):
    return [pltpu.with_memory_space_constraint(a, pltpu.HBM) for a in arrays]


def spread(*arrays):
    return pl.pallas_call(
        spread_kernel,
        out_shape=(
            jax.ShapeDtypeStruct((OWNERS * ROWS, WIDTH), F32),
            jax.ShapeDtypeStruct((2, PERIODS, OWNERS // 2, 8, 128), jnp.int32),
            jax.ShapeDtypeStruct((2, PERIODS, OWNERS // 2, 8, 128), F32),
        ),
        in_specs=[HBM] * 5,
        out_specs=[VMEM] * 3,
        scratch_shapes=[
            pltpu.VMEM((ROWS, WIDTH), F32),
            pltpu.VMEM((1, ROWS), jnp.int32),
            pltpu.VMEM((1, ROWS), jnp.int32),
            pltpu.VMEM((1, ROWS), F32),
            pltpu.VMEM((OWNERS, 1, 128), jnp.int32),
            pltpu.VMEM((OWNERS, ROWS, WIDTH), BF16),
            pltpu.VMEM((OWNERS, 1, 128), jnp.int32),
            pltpu.SemaphoreType.DMA((5,)),
            pltpu.SemaphoreType.DMA((2, 2 * Gather.OPS)),
            pltpu.SemaphoreType.DMA((2, OWNERS)),
            pltpu.SemaphoreType.DMA((2, 2, 32)),
        ],
        compiler_params=pltpu.CompilerParams(
            collective_id=0, has_side_effects=True, vmem_limit_bytes=28 * 2**20
        ),
        name="spread",
    )(*in_hbm(*arrays))


def message_kernel(
    wide, meta, time, freq_h, weight_h, bias_h, memory_h, totals, counts,
    freq, weight, bias, memory, windows, window_times, pieces, rows_v, rows_s, index_v, index_s,
    segments, parts, gathered, sem, index_sems, load_sems,
):
    t = lax.axis_index("tm")
    bucket = lax.axis_index("node") * PERIODS + t
    mine = pl.ds(pl.multiple_of(t * SHARE, SHARE), SHARE)
    loads = [
        pltpu.make_async_copy(src, dst, load_sems.at[i])
        for i, (src, dst) in enumerate(
            ((freq_h, freq), (weight_h, weight), (bias_h, bias), (memory_h.at[mine], memory))
        )
    ]
    for load in loads:
        load.start()
    totals[...] = jnp.zeros_like(totals)
    counts[...] = jnp.zeros_like(counts)
    gathered[...] = jnp.zeros_like(gathered)
    start_parts, end_parts = [], []
    for i in range(8):
        own = meta[pl.ds(32 * i, 32)] >> 20
        start_parts.append(jnp.sum(jnp.where(own < bucket, 1.0, 0.0), axis=1))
        end_parts.append(jnp.sum(jnp.where(own <= bucket, 1.0, 0.0), axis=1))
    ones_row = jnp.ones((8, 128), BF16)
    start = dot(ones_row, jnp.concatenate(start_parts, 0).astype(BF16), NT)
    end = dot(ones_row, jnp.concatenate(end_parts, 0).astype(BF16), NT)
    upper = where01(iota((BLOCKS, BLOCKS), 0) < iota((BLOCKS, BLOCKS), 1))
    ones_wide = jnp.ones((8, BLOCKS), BF16)
    ones_col = jnp.ones((BLOCKS, 128), BF16)
    ones_term = jnp.ones((CHUNK, 128), BF16)
    longest = jnp.max(end - start)
    for load in loads:
        load.wait()
    own_rows = memory[...].astype(BF16)
    own_rows = jnp.concatenate([own_rows, jnp.zeros((128 - SHARE, WIDTH), BF16)], 0)
    freqs = jnp.broadcast_to(freq[...], (CHUNK, 128))

    def index_copy(ch):
        return pltpu.make_async_copy(index_v.at[ch], index_s.at[ch], index_sems.at[ch])

    def one_round(r, carry):
        begin = start + (r * 128).astype(F32)
        size = jnp.clip(end - begin, 0.0, 128.0)
        before = dot(size.astype(BF16), upper)
        which = iota((8, BLOCKS), 0)
        begin_i = begin.astype(jnp.int32)
        rows_v[...] = jnp.where(which == 0, begin_i, (before + size).astype(jnp.int32))
        copy = pltpu.make_async_copy(rows_v, rows_s, sem)
        copy.start()
        copy.wait()
        total = rows_s[1, BLOCKS - 1]

        def fetch(i, carry):
            for u in range(8):
                b = i * 8 + u
                at = rows_s[0, b] >> 7
                for j in range(2):
                    from_row = pl.ds(jnp.minimum(at + j, 7), 1)
                    windows[j, pl.ds(b, 1), :] = meta[b, from_row, :]
                    window_times[j, pl.ds(b, 1), :] = time[b, from_row, :]
            return carry

        lax.fori_loop(0, BLOCKS // 8, fetch, 0)
        for j in range(2):
            m = windows[j]
            w = window_times[j]
            period = (iota((BLOCKS, 128), 0) >> 4) & 7
            seg = period * SHARE + ((m >> 14) & 63) - 256
            t1 = w.astype(BF16).astype(F32)
            t2 = (w - t1).astype(BF16).astype(F32)
            t3 = w - t1 - t2
            for k, piece in enumerate(
                (seg.astype(F32), ((m >> 6) & 255).astype(F32), (m & 63).astype(F32), t1, t2, t3)
            ):
                pieces[:, 256 * k + 128 * j : 256 * k + 128 * (j + 1)] = piece.astype(BF16)
        offset = (begin_i & 127).astype(F32) - before

        def one_group(group, carry):
            first = group * GROUP * CHUNK

            def locate(ch, carry):
                at = first + ch * CHUNK
                p = (at + iota((CHUNK, BLOCKS), 0)).astype(F32)
                low = jnp.broadcast_to(before[0:1], (CHUNK, BLOCKS))
                high = low + jnp.broadcast_to(size[0:1], (CHUNK, BLOCKS))
                hit = (low <= p) & (p < high)
                shift = jnp.sum(
                    jnp.where(hit, jnp.broadcast_to(offset[0:1], (CHUNK, BLOCKS)), 0.0),
                    axis=1,
                    keepdims=True,
                )
                found = dot(where01(hit), pieces[...])
                here = (p + shift) == iota((CHUNK, BLOCKS), 1).astype(F32)
                chosen = [
                    jnp.where(here, found[:, 256 * k : 256 * (k + 1)], 0.0).astype(BF16)
                    for k in range(6)
                ]
                other = dot(ones_wide, chosen[1], NT) * 64.0 + dot(ones_wide, chosen[2], NT)
                index_v[ch] = other.astype(jnp.int32)
                index_copy(ch).start()
                seg_row = dot(ones_wide, chosen[0], NT) + 256.0
                lane_p = at + iota((8, CHUNK), 1)
                segments[ch] = jnp.where(lane_p < total, seg_row, -1.0)
                seg_col = dot(chosen[0], ones_col).astype(jnp.int32) + 256
                own_hot = where01((seg_col & 63) == iota((CHUNK, 128), 1))
                own = dot(own_hot, own_rows).astype(BF16)
                moment = (
                    dot(chosen[3], ones_col) + dot(chosen[4], ones_col) + dot(chosen[5], ones_col)
                )
                encoding = cosine(moment * freqs).astype(BF16)
                parts[ch] = dot(own, weight[pl.ds(0, WIDTH), :]) + dot(
                    encoding, weight[pl.ds(2 * WIDTH, 128), :]
                )
                parts[ch] = parts[ch] + bias[...]
                return carry

            def collect(ch, carry):
                index_copy(ch).wait()

                def pick(i, carry):
                    for u in range(UNROLL):
                        q = i * UNROLL + u
                        gathered[pl.ds(q, 1), :] = wide[pl.ds(index_s[ch, 0, q], 1), :]
                    return carry

                left = jnp.minimum(total - first - ch * CHUNK, CHUNK)
                lax.fori_loop(0, (left + UNROLL - 1) // UNROLL, pick, 0)
                other = dot(gathered[...].astype(BF16), weight[pl.ds(WIDTH, WIDTH), :])
                message = jnp.maximum(parts[ch] + other, 0.0)
                seg_hot = where01(
                    iota((ROWS, CHUNK), 0).astype(F32)
                    == jnp.broadcast_to(segments[ch, 0:1, :], (ROWS, CHUNK))
                )
                upper_part = message.astype(BF16)
                lower_part = (message - upper_part.astype(F32)).astype(BF16)
                totals[...] += dot(seg_hot, upper_part) + dot(seg_hot, lower_part)
                counts[...] += dot(seg_hot, ones_term)
                return carry

            chunks = jnp.minimum((total - first + CHUNK - 1) // CHUNK, GROUP)
            lax.fori_loop(0, chunks, locate, 0)
            lax.fori_loop(0, chunks, collect, 0)
            return carry

        lax.fori_loop(0, (total + GROUP * CHUNK - 1) // (GROUP * CHUNK), one_group, 0)
        return carry

    rounds = (longest.astype(jnp.int32) + 127) // 128
    lax.fori_loop(0, rounds, one_round, 0)


def messages(wide, meta, time, *others):
    return pl.pallas_call(
        message_kernel,
        out_shape=(
            jax.ShapeDtypeStruct((ROWS, WIDTH), F32),
            jax.ShapeDtypeStruct((ROWS, 128), F32),
        ),
        in_specs=[VMEM] * 3 + [HBM] * 4,
        out_specs=[VMEM] * 2,
        scratch_shapes=[
            pltpu.VMEM((1, 128), F32),
            pltpu.VMEM((2 * WIDTH + 128, WIDTH), BF16),
            pltpu.VMEM((1, WIDTH), F32),
            pltpu.VMEM((SHARE, WIDTH), F32),
            pltpu.VMEM((2, BLOCKS, 128), jnp.int32),
            pltpu.VMEM((2, BLOCKS, 128), F32),
            pltpu.VMEM((BLOCKS, 6 * 256), BF16),
            pltpu.VMEM((8, BLOCKS), jnp.int32),
            pltpu.SMEM((8, BLOCKS), jnp.int32),
            pltpu.VMEM((GROUP, 8, CHUNK), jnp.int32),
            pltpu.SMEM((GROUP, 8, CHUNK), jnp.int32),
            pltpu.VMEM((GROUP, 8, CHUNK), F32),
            pltpu.VMEM((GROUP, CHUNK, WIDTH), F32),
            pltpu.VMEM((CHUNK, WIDTH), F32),
            pltpu.SemaphoreType.DMA,
            pltpu.SemaphoreType.DMA((GROUP,)),
            pltpu.SemaphoreType.DMA((4,)),
        ],
        compiler_params=pltpu.CompilerParams(vmem_limit_bytes=16 * 2**20),
        name="messages",
    )(wide, meta, time, *in_hbm(*others))


def update_kernel(
    totals, counts, memory_h, weight_h, bias_h, arrived, final, memory, weight, bias, history,
    load_sems, sems,
):
    t = lax.axis_index("tm")
    o = lax.axis_index("node")
    mine = pl.ds(pl.multiple_of(t * SHARE, SHARE), SHARE)
    loads = [
        pltpu.make_async_copy(src, dst, load_sems.at[i])
        for i, (src, dst) in enumerate(
            ((memory_h.at[mine], memory), (weight_h, weight), (bias_h, bias))
        )
    ]
    for load in loads:
        load.start()
    barrier = pltpu.get_barrier_semaphore()
    for k in range(1, PERIODS):
        pl.semaphore_signal(
            barrier, inc=1, device_id=(lax.rem(t + k, PERIODS), o), device_id_type=MESH
        )
    count = counts[...]
    count = jnp.concatenate([count, count], 1)
    mean = (totals[...] / jnp.maximum(count, 1.0)).astype(BF16)
    for load in loads:
        load.wait()
    gates = dot(mean, weight[...])
    rate = jax.nn.sigmoid(gates[:, :WIDTH] + bias[...])
    candidate = jnp.tanh(gates[:, WIDTH:])
    touched = count > 0.0
    keep = jnp.where(touched, 1.0 - rate, 1.0)
    write = jnp.where(touched, rate * candidate, 0.0)
    state = memory[...]
    for k in range(PERIODS):
        rows = slice(k * SHARE, (k + 1) * SHARE)
        state = keep[rows] * state + write[rows]
        history[k] = state.astype(BF16)

        @pl.when(t == k)
        def _():
            final[...] = state

    pl.semaphore_wait(barrier, PERIODS - 1)
    copies = []
    for k in (4, 3, 5, 2, 6, 1, 7):
        to = lax.rem(t + k, PERIODS)
        copy = pltpu.make_async_remote_copy(
            src_ref=history.at[to],
            dst_ref=arrived.at[t],
            send_sem=sems.at[0, k],
            recv_sem=sems.at[1, k],
            device_id=(to, o),
            device_id_type=MESH,
        )
        copy.start()
        copies.append(copy)
    arrived[pl.ds(t, 1)] = history[pl.ds(t, 1)]
    for copy in copies:
        copy.wait()


def update(totals, counts, memory, weight, bias):
    return pl.pallas_call(
        update_kernel,
        out_shape=(
            jax.ShapeDtypeStruct((PERIODS, SHARE, WIDTH), BF16),
            jax.ShapeDtypeStruct((SHARE, WIDTH), F32),
        ),
        in_specs=[VMEM] * 2 + [HBM] * 3,
        out_specs=[VMEM] * 2,
        scratch_shapes=[
            pltpu.VMEM((SHARE, WIDTH), F32),
            pltpu.VMEM((WIDTH, 2 * WIDTH), BF16),
            pltpu.VMEM((1, WIDTH), F32),
            pltpu.VMEM((PERIODS, SHARE, WIDTH), BF16),
            pltpu.SemaphoreType.DMA((3,)),
            pltpu.SemaphoreType.DMA((2, PERIODS)),
        ],
        compiler_params=pltpu.CompilerParams(
            collective_id=1, has_side_effects=True, vmem_limit_bytes=16 * 2**20
        ),
        name="update",
    )(totals, counts, *in_hbm(memory, weight, bias))


def shards(
    memory,
    src_slot,
    dst_slot,
    event_time,
    touched_rows,
    time_freq,
    msg_weight,
    msg_bias,
    gate_weight,
    update_bias,
):
    wide, meta, time = spread(
        memory,
        src_slot[0],
        dst_slot[0],
        event_time[0],
        touched_rows.reshape(OWNERS, 1, 128),
    )
    totals, counts = messages(
        wide,
        meta.reshape(BLOCKS, 8, 128),
        time.reshape(BLOCKS, 8, 128),
        time_freq[None],
        msg_weight,
        msg_bias[None],
        memory,
    )
    arrived, final = update(totals, counts, memory, gate_weight, update_bias[None])
    mine = lax.broadcasted_iota(jnp.int32, (PERIODS, SHARE, WIDTH), 0) == lax.axis_index("tm")
    result = jnp.where(mine, final[None], arrived.astype(F32))
    return result.reshape(1, ROWS, WIDTH)


def solution(mesh):
    return jax.shard_map(
        shards,
        mesh=mesh,
        in_specs=(
            P("node", None),
            P("tm", "node", None),
            P("tm", "node", None),
            P("tm", "node", None),
            P("tm", "node", None, None),
            P(),
            P(),
            P(),
            P(),
            P(),
        ),
        out_specs=P("tm", "node", None),
        check_vma=False,
    )
```

time: 101 us -> 76.6 us (0.76)
  the two profiles are of different devices: /device:TPU:4 before, /device:TPU:1 now
where the time goes in v2:
time: 76.6 us; the launch traced here: 76.3 us
  Pallas kernels  75.4 us (98%)
  other arithmetic  0.91 us (1%)
    pallas_call x1, Pallas kernels, spread(): pl.pallas_call(spread_kernel, out_shape=(jax.ShapeDtypeStruct((OWNERS * R...  45.8 us
    pallas_call x1, Pallas kernels, messages(): pl.pallas_call(message_kernel, out_shape=(jax.ShapeDtypeStruct((ROWS, WID...  17.1 us
    pallas_call x1, Pallas kernels, update(): pl.pallas_call(update_kernel, out_shape=(jax.ShapeDtypeStruct((PERIODS, S...  12.5 us

profile of v2, /device:TPU:1, one launch (start us, length us, event | category | flops | bytes accessed | tf_op | source)
XLA Modules:
  0.0 76.3 jit_solution(7221725786064781578)
XLA Ops:
  0.0 45.8 %spread.1 = (f32[16384,256]{1,0:T(8,128)S(1)}, s32[2,8,16,8,128]{4,3,2,1,0:T(8,128)S(1)}, f32[2,8,16,8,128]{4,3,2,1,0:T(8,128)S(1)}) custom-call(f32[512,256]{1,0:T(8,128)} %memory_h.5, s32[1,512]{1,0:T(1,128)} %bitcast.13, s32[1,512]{1,0:T(1,128)} %bitcast.14, f32[1,512]{1,0:T(1,128)} %bitcast.15, s32[32,1,128]{2,1,0:T(1,128)} %bitcast.12), custom_call_target="tpu_custom_call" | custom-call | tf_op jit(solution)/shard_map/spread/pallas_call | solution.py:409
  45.9 17.1 %messages.1 = (f32[512,256]{1,0:T(8,128)S(1)}, f32[512,128]{1,0:T(8,128)S(1)}) custom-call(f32[16384,256]{1,0:T(8,128)S(1)} %get-tuple-element.12.wide, s32[256,8,128]{2,1,0:T(8,128)S(1)} %bitcast.10, f32[256,8,128]{2,1,0:T(8,128)S(1)} %bitcast.11, f32[1,128]{1,0:T(1,128)} %bitcast.18, bf16[640,256]{1,0:T(8,128)(2,1)} %weight_h.2, f32[1,256]{1,0:T(1,128)} %bitcast.16, ...), custom_call_target="tpu_custom_call" | custom-call | tf_op jit(solution)/shard_map/messages/pallas_call | solution.py:591
  62.9 12.5 %update.1 = (bf16[8,64,256]{2,1,0:T(8,128)(2,1)S(1)}, f32[64,256]{1,0:T(8,128)S(1)}) custom-call(f32[512,256]{1,0:T(8,128)S(1)} %get-tuple-element.15.totals, f32[512,128]{1,0:T(8,128)S(1)} %get-tuple-element.16.counts, f32[512,256]{1,0:T(8,128)} %memory_h.5, bf16[256,512]{1,0:T(8,128)(2,1)} %weight_h.3, f32[1,256]{1,0:T(1,128)} %bitcast.17), custom_call_target="tpu_custom_call" | custom-call | tf_op jit(solution)/shard_map/update/pallas_call | solution.py:684
  75.4 0.9 %convert_select_fusion = f32[8,64,256]{2,1,0:T(8,128)} fusion(bf16[8,64,256]{2,1,0:T(8,128)(2,1)S(1)} %get-tuple-element.18, f32[64,256]{1,0:T(8,128)S(1)} %get-tuple-element.17, pred[8]{0:T(512)(128)(4,1)S(1)} %iota_compare_fusion), kind=kLoop, calls=%fused_computation | loop fusion | flops 262144 | bytes 851976 | tf_op jit(solution)/shard_map/jit(_where)/select_n | solution.py:737
  (1 shorter events, 0.0 us)
